TPU v7x, 32 devices: a whole 2x2x4 slice. The times are simulated.
32 devices in a mesh: section: 2 (over core), seq: 4 (over y, x), mp: 4 (over z).
Axes of the slice: x: 2, y: 2, z: 4, core: 2. Of those that a mesh axis runs over, the one named last changes fastest.
Arguments:
- token_ids: int32 [2, 1024], P(None, 'seq'), may hold values from 0 to 511
- embed_table: bfloat16 [512, 4096], P(None, 'mp'), may hold values from -40 to 40
- norm_gain: bfloat16 [2, 4096], P('section', 'mp'), may hold values from 0.099609375 to 1.8984375
- short_filters: bfloat16 [2, 3, 7, 4096], P('section', None, None, 'mp'), may hold values from -2 to 2
- medium_filters: bfloat16 [2, 128, 4096], P('section', None, 'mp'), may hold values from -0.5 to 0.5
- out_weight: bfloat16 [2, 4096, 4096], P('section', 'seq', 'mp'), may hold values from -0.09375 to 0.09375
Outputs:
- streams: bfloat16 [2, 2, 1024, 4096], P('section', None, 'seq', 'mp')
All inputs are finite; a program needn't handle non-finite values.
Results may differ from a plain program's by a relative error of at most 0.018.
Values may be sent and summed in bfloat16 or wider, within the bound.
A program may use at most 64 MiB of HBM per device.

v0:
```python
import jax
import jax.numpy as jnp
from jax import lax
from jax.sharding import PartitionSpec as P

D = 4096


def passed_along(value, axis, by):
    devices = lax.axis_size(axis)
    pairs = [(i, i + by) for i in range(devices) if 0 <= i + by < devices]
    return lax.ppermute(value, axis, pairs)


def depthwise(extended, taps):
    kernel = jnp.flip(taps, 0)[:, None, :]
    result = lax.conv_general_dilated(
        extended[None],
        kernel,
        (1,),
        "VALID",
        dimension_numbers=("NWC", "WIO", "NWC"),
        feature_group_count=taps.shape[1],
        preferred_element_type=jnp.float32,
    )
    return result[0]


def mixer_layer(stream_in, gain, shorts, medium, weight_cols):
    rows = stream_in.shape[0]
    stream = stream_in.astype(jnp.float32)
    own_squares = jnp.sum(stream * stream, axis=1, keepdims=True)
    all_squares = lax.psum(own_squares, "mp")
    normed = (
        stream * lax.rsqrt(all_squares / D + 1e-06) * gain.astype(jnp.float32)[None, :]
    ).astype(jnp.bfloat16)
    short_span = shorts.shape[1] - 1
    medium_span = medium.shape[0] - 1
    lower_rim = passed_along(normed[rows - short_span :], "seq", 1)
    extended = jnp.concatenate([lower_rim, normed], axis=0)
    features = [depthwise(extended, shorts[index]).astype(jnp.bfloat16) for index in range(3)]
    product = (features[1].astype(jnp.float32) * features[2].astype(jnp.float32)).astype(
        jnp.bfloat16
    )
    product_rim = passed_along(product[rows - medium_span :], "seq", 1)
    filtered = depthwise(jnp.concatenate([product_rim, product], axis=0), medium)
    query = features[0]
    gated = (query.astype(jnp.float32) * filtered).astype(jnp.bfloat16)
    empty = jnp.zeros((rows, weight_cols.shape[1]), jnp.float32)
    piece = jax.tree.map(lambda a: lax.all_gather(a, "mp", axis=1, tiled=True), gated)
    block_rows = lax.slice_in_dim(weight_cols, 0, piece.shape[1], axis=0)
    projected = empty + jnp.dot(piece, block_rows, preferred_element_type=jnp.float32)
    return (stream + projected).astype(jnp.bfloat16)


def local(token_ids, embed_table, norm_gain, short_filters, medium_filters, out_weight):
    section_index = lax.axis_index("section")
    weight_cols = lax.all_gather(out_weight, "seq", axis=1, tiled=True)[0]
    gain = norm_gain[0]
    shorts = short_filters[0]
    medium = medium_filters[0]
    micro_count = token_ids.shape[0]
    rows = token_ids.shape[1]
    width = embed_table.shape[1]
    vocab_ids = lax.broadcasted_iota(jnp.int32, (rows, embed_table.shape[0]), 1)
    received = jnp.zeros((rows, width), jnp.bfloat16)
    results = []
    for tick_index in range(micro_count + 1):
        chosen = token_ids[min(tick_index, micro_count - 1)]
        one_hot = (chosen[:, None] == vocab_ids).astype(jnp.bfloat16)
        embedded = jnp.dot(one_hot, embed_table, preferred_element_type=jnp.float32).astype(
            jnp.bfloat16
        )
        stream_in = jnp.where(section_index == 0, embedded, received)
        result = mixer_layer(stream_in, gain, shorts, medium, weight_cols)
        results.append(result)
        if tick_index < micro_count:
            received = passed_along(result, "section", 1)
    ordered = [
        jnp.where(section_index == 0, results[index], results[index + 1])
        for index in range(micro_count)
    ]
    return jnp.stack(ordered)[None]


def solution(mesh):
    in_specs = (
        P(None, "seq"),
        P(None, "mp"),
        P("section", "mp"),
        P("section", None, None, "mp"),
        P("section", None, "mp"),
        P("section", "seq", "mp"),
    )
    out_specs = P("section", None, "seq", "mp")
    return jax.shard_map(local, mesh=mesh, in_specs=in_specs, out_specs=out_specs, check_vma=False)
```

profile of v0, /device:TPU:0, one launch (start us, length us, event | category | flops | bytes accessed | tf_op | source)
XLA Modules:
  0.0 514.0 jit_solution(5375181700684785683)
XLA Ops:
  6.5 0.8 fusion.139
  7.3 0.7 mul.112
  8.0 0.6 fusion.101
  8.6 13.5 %psum.21 = f32[256,1]{0,1:T(1,128)S(1)} all-reduce(f32[256,1]{0,1:T(1,128)S(1)} %bitcast.136), channel_id=1, replica_groups=mesh['section'=2,'seq'=4,'mp'=4] {'mp'}, use_global_device_ids=true, to_apply=%region_1.2 | all-reduce | flops 256 | bytes 2048 | tf_op jit(solution)/shard_map/psum | solution.py:33
  22.3 3.4 collective-permute-start
  26.5 2.6 rev.25
  29.5 0.3 copy.26
  30.0 0.6 fusion.25
  30.6 0.7 fusion.23
  31.2 0.3 copy.32
  31.7 0.8 slice_bitcast_fusion.5
  32.5 4.1 collective-permute-start.1
  36.6 0.6 fusion.19
  37.2 0.6 copy.28
  37.9 2.3 reshape.126
  40.2 1.2 maximum_bitcast_fusion.1
  41.5 15.2 %fusion.86 = bf16[1,256,1024]{2,0,1:T(2,128)(2,1)} fusion(bf16[1,383,1024]{2,1,0:T(8,128)(2,1)S(1)} %maximum_bitcast_fusion.1, f32[1,264,1024]{2,0,1:T(1,128)S(1)} %copy-done.2, bf16[128,1,1024]{2,0,1:T(8,128)(2,1)S(1)} %bitcast.116), kind=kOutput, calls=%fused_computation.73 | convolution fusion | flops 67633152 | bytes 2619392 | tf_op jit(solution)/shard_map/conv_general_dilated | solution.py:17
  56.7 0.7 all-gather.8.cloned.1.call-update
  57.5 0.5 all-gather.12.cloned.1.call-start
  58.0 78.3 %all-gather.10.cloned.1.call-done = bf16[1,256,4096]{2,0,1:T(2,128)(2,1)} async-done(((bf16[1,256,1024]{2,0,1:T(2,128)(2,1)}), bf16[1,256,4096]{2,0,1:T(2,128)(2,1)}) %all-gather.10.cloned.1.call-update) | async-done | bytes 2097168 | tf_op jit(solution)/shard_map/all_gather | solution.py:50
  136.3 87.5 %all-gather.8.cloned.1.call-done = bf16[1,4096,1024]{2,1,0:T(8,128)(2,1)} async-done(((bf16[1,1024,1024]{2,1,0:T(8,128)(2,1)}), bf16[1,4096,1024]{2,1,0:T(8,128)(2,1)}) %all-gather.8.cloned.1.call-update) | async-done | bytes 8388624 | tf_op jit(solution)/shard_map/all_gather | solution.py:58
  223.8 8.6 %fusion.54 = bf16[256,1024]{1,0:T(8,128)(2,1)S(1)} fusion(bf16[1,4096,1024]{2,1,0:T(8,128)(2,1)} %all-gather.8.cloned.1.call-done, bf16[1,256,4096]{2,0,1:T(2,128)(2,1)} %all-gather.10.cloned.1.call-done, bf16[256,1024]{1,0:T(8,128)(2,1)S(1)} %get-tuple-element.15), kind=kOutput, calls=%fused_computation.62 | convolution fusion | flops 2148270080 | bytes 11534336 | tf_op jit(solution)/shard_map/dot_general | solution.py:52
  232.5 1.6 collective-permute-start.2
  234.1 1.5 collective-permute-done.2
  235.6 0.6 fusion.104
  236.2 11.7 %psum.22 = f32[256,1]{0,1:T(1,128)S(1)} all-reduce(f32[256,1]{0,1:T(1,128)S(1)} %bitcast.135), channel_id=1, replica_groups=mesh['section'=2,'seq'=4,'mp'=4] {'mp'}, use_global_device_ids=true, to_apply=%region_3.4 | all-reduce | flops 256 | bytes 2048 | tf_op jit(solution)/shard_map/psum | solution.py:33
  248.1 3.4 collective-permute-start.3
  251.5 1.4 collective-permute-done.3
  253.3 0.3 copy.36
  253.6 0.6 fusion.33
  254.2 0.7 fusion.31
  254.9 0.3 copy.42
  255.4 0.8 slice_bitcast_fusion.4
  256.2 4.9 collective-permute-start.4
  261.1 0.6 fusion.27
  261.7 0.6 copy.38
  262.3 1.3 reshape.127
  263.7 0.9 collective-permute-done.4
  264.6 1.1 maximum_bitcast_fusion.2
  265.7 15.2 %fusion.92 = bf16[1,256,1024]{2,0,1:T(2,128)(2,1)} fusion(bf16[1,383,1024]{2,1,0:T(8,128)(2,1)S(1)} %maximum_bitcast_fusion.2, f32[1,264,1024]{2,0,1:T(1,128)S(1)} %reshape.127, bf16[128,1,1024]{2,0,1:T(8,128)(2,1)S(1)} %bitcast.117), kind=kOutput, calls=%fused_computation.75 | convolution fusion | flops 67633152 | bytes 2619392 | tf_op jit(solution)/shard_map/conv_general_dilated | solution.py:17
  281.1 80.5 %all-gather.12.cloned.1.call-done = bf16[1,256,4096]{2,0,1:T(2,128)(2,1)} async-done(((bf16[1,256,1024]{2,0,1:T(2,128)(2,1)}), bf16[1,256,4096]{2,0,1:T(2,128)(2,1)}) %all-gather.12.cloned.1.call-update) | async-done | bytes 2097168 | tf_op jit(solution)/shard_map/all_gather | solution.py:50
  361.6 8.6 %fusion.59 = bf16[256,1024]{1,0:T(8,128)(2,1)S(1)} fusion(bf16[1,4096,1024]{2,1,0:T(8,128)(2,1)} %all-gather.8.cloned.1.call-done, bf16[1,256,4096]{2,0,1:T(2,128)(2,1)} %all-gather.12.cloned.1.call-done, bf16[256,1024]{1,0:T(8,128)(2,1)S(1)} %copy-done.4), kind=kOutput, calls=%fused_computation.63 | convolution fusion | flops 2148270080 | bytes 11534336 | tf_op jit(solution)/shard_map/dot_general | solution.py:52
  370.2 1.3 collective-permute-start.5
  371.6 1.5 collective-permute-done.5
  373.1 0.3 fusion.107
  373.3 9.4 %psum.23 = f32[256,1]{0,1:T(1,128)S(1)} all-reduce(f32[256,1]{0,1:T(1,128)S(1)} %bitcast.131), channel_id=1, replica_groups=mesh['section'=2,'seq'=4,'mp'=4] {'mp'}, use_global_device_ids=true, to_apply=%region_5.6 | all-reduce | flops 256 | bytes 2048 | tf_op jit(solution)/shard_map/psum | solution.py:33
  382.9 3.4 collective-permute-start.6
  386.3 1.4 collective-permute-done.6
  388.1 0.3 copy.46
  388.4 0.6 fusion.41
  389.1 0.7 fusion.39
  389.7 0.3 copy.52
  390.2 0.8 slice_bitcast_fusion.3
  391.0 5.1 collective-permute-start.7
  396.1 0.6 fusion.35
  396.7 0.6 copy.48
  397.4 1.3 reshape.128
  398.7 0.7 collective-permute-done.7
  399.4 1.1 maximum_bitcast_fusion.3
  400.5 15.2 %fusion.98 = bf16[1,256,1024]{2,0,1:T(2,128)(2,1)} fusion(bf16[1,383,1024]{2,1,0:T(8,128)(2,1)S(1)} %maximum_bitcast_fusion.3, f32[1,264,1024]{2,0,1:T(1,128)S(1)} %reshape.128, bf16[128,1,1024]{2,0,1:T(8,128)(2,1)S(1)} %bitcast.118), kind=kOutput, calls=%fused_computation.77 | convolution fusion | flops 67633152 | bytes 2619392 | tf_op jit(solution)/shard_map/conv_general_dilated | solution.py:17
  415.7 1.0 copy-done.6
  416.9 80.5 %all-gather.14.cloned.1.call-done = bf16[1,256,4096]{2,0,1:T(2,128)(2,1)} async-done(((bf16[1,256,1024]{2,0,1:T(2,128)(2,1)}), bf16[1,256,4096]{2,0,1:T(2,128)(2,1)}) %all-gather.14.cloned.1.call-update) | async-done | bytes 2097168 | tf_op jit(solution)/shard_map/all_gather | solution.py:50
  497.4 8.7 %fusion.78 = bf16[1,256,1024]{2,1,0:T(8,128)(2,1)S(1)} fusion(bf16[256,1024]{1,0:T(8,128)(2,1)S(1)} %copy-done.8, bf16[1,4096,1024]{2,1,0:T(8,128)(2,1)} %all-gather.8.cloned.1.call-done, bf16[1,256,4096]{2,0,1:T(2,128)(2,1)} %all-gather.14.cloned.1.call-done, bf16[256,1024]{1,0:T(8,128)(2,1)S(1)} %get-tuple-element.6, pred[]{:T(512)S(6)} %eq.14), kind=kOutput, calls=%fused_computation.71 | convolution fusion | flops 2148532224 | bytes 12058625 | tf_op jit(solution)/shard_map/dot_general | solution.py:52
  506.1 1.1 maximum_bitcast_fusion
  (69 shorter events, 4.0 us)
Async XLA Ops:
  6.5 1.5 copy-start
  6.5 129.7 %all-gather.10.cloned.1.call-start = ((), (), s32[]{:S(2)}) async-start(), calls=%async_computation.1 | async-start | bytes 5242880 | tf_op jit(solution)/shard_map/all_gather | solution.py:50
  8.0 17.7 %copy-start.13 = (bf16[1,3,7,1024]{3,2,1,0:T(8,128)(2,1)S(1)}, bf16[1,3,7,1024]{3,2,1,0:T(8,128)(2,1)}, u32[]{:S(2)}) copy-start(bf16[1,3,7,1024]{3,2,1,0:T(8,128)(2,1)} %param.9) | copy-start | bytes 129028
  8.0 18.5 %copy-start.9 = (bf16[1,128,1024]{2,1,0:T(8,128)(2,1)S(1)}, bf16[1,128,1024]{2,1,0:T(8,128)(2,1)}, u32[]{:S(2)}) copy-start(bf16[1,128,1024]{2,1,0:T(8,128)(2,1)} %param.10) | copy-start | bytes 786436
  22.3 6.8 %collective-permute-start = (bf16[6,1024]{1,0:T(8,128)(2,1)S(1)}, bf16[6,1024]{1,0:T(8,128)(2,1)S(1)}, u32[]{:S(2)}, u32[]{:S(2)}) collective-permute-start(bf16[6,1024]{1,0:T(8,128)(2,1)S(1)} %slice.84), channel_id=1, source_target_pairs={{0,4},{4,8},{8,12},{1,5},{5,9},{9,13},{2,6},{6,10},{10,14},{3,7},{... | collective-permute-start | bytes 36872 | tf_op jit(solution)/shard_map/ppermute | solution.py:12
  29.3 0.7 copy-start.14
  32.5 7.7 %collective-permute-start.1 = (bf16[127,1024]{1,0:T(8,128)(2,1)}, bf16[127,1024]{1,0:T(8,128)(2,1)}, u32[]{:S(2)}, u32[]{:S(2)}) collective-permute-start(bf16[127,1024]{1,0:T(8,128)(2,1)} %slice_bitcast_fusion.5), channel_id=1, source_target_pairs={{0,4},{4,8},{8,12},{1,5},{5,9},{9,13},{2,6},{6,10},{10,14},{3,7},{... | collective-permute-start | bytes 780296 | tf_op jit(solution)/shard_map/ppermute | solution.py:12
  40.2 1.3 copy-start.2
  40.2 1.4 copy-start.10
  56.7 167.1 %all-gather.8.cloned.1.call-start = ((), (), s32[]{:S(2)}) async-start(), calls=%async_computation | async-start | bytes 10485760 | tf_op jit(solution)/shard_map/all_gather | solution.py:58
  57.5 304.1 %all-gather.12.cloned.1.call-start = ((), (), s32[]{:S(2)}) async-start(), calls=%async_computation.2 | async-start | bytes 5242880 | tf_op jit(solution)/shard_map/all_gather | solution.py:50
  232.5 3.1 copy-start.5
  232.5 3.1 collective-permute-start.2
  236.2 16.7 %copy-start.3 = (bf16[256,1024]{1,0:T(8,128)(2,1)}, bf16[256,1024]{1,0:T(8,128)(2,1)S(1)}, u32[]{:S(2)}) copy-start(bf16[256,1024]{1,0:T(8,128)(2,1)S(1)} %get-tuple-element.8) | copy-start | bytes 1572868
  248.1 4.8 collective-permute-start.3
  256.2 8.4 %collective-permute-start.4 = (bf16[127,1024]{1,0:T(8,128)(2,1)}, bf16[127,1024]{1,0:T(8,128)(2,1)}, u32[]{:S(2)}, u32[]{:S(2)}) collective-permute-start(bf16[127,1024]{1,0:T(8,128)(2,1)} %slice_bitcast_fusion.4), channel_id=1, source_target_pairs={{0,4},{4,8},{8,12},{1,5},{5,9},{9,13},{2,6},{6,10},{10,14},{3,7},{... | collective-permute-start | bytes 780296 | tf_op jit(solution)/shard_map/ppermute | solution.py:12
  263.6 2.0 copy-start.11
  265.6 95.9 %copy-start.4 = (bf16[256,1024]{1,0:T(8,128)(2,1)S(1)}, bf16[256,1024]{1,0:T(8,128)(2,1)}, u32[]{:S(2)}) copy-start(bf16[256,1024]{1,0:T(8,128)(2,1)} %copy-done.3) | copy-start | bytes 1572868
  280.9 216.5 %all-gather.14.cloned.1.call-start = ((), (), s32[]{:S(2)}) async-start(), calls=%async_computation.3 | async-start | bytes 5242880 | tf_op jit(solution)/shard_map/all_gather | solution.py:50
  370.2 12.7 %copy-start.7 = (bf16[256,1024]{1,0:T(8,128)(2,1)}, bf16[256,1024]{1,0:T(8,128)(2,1)S(1)}, u32[]{:S(2)}) copy-start(bf16[256,1024]{1,0:T(8,128)(2,1)S(1)} %fusion.59) | copy-start | bytes 1572868
  370.2 2.8 collective-permute-start.5
  382.9 4.8 collective-permute-start.6
  391.0 8.4 %collective-permute-start.7 = (bf16[127,1024]{1,0:T(8,128)(2,1)}, bf16[127,1024]{1,0:T(8,128)(2,1)}, u32[]{:S(2)}, u32[]{:S(2)}) collective-permute-start(bf16[127,1024]{1,0:T(8,128)(2,1)} %slice_bitcast_fusion.3), channel_id=1, source_target_pairs={{0,4},{4,8},{8,12},{1,5},{5,9},{9,13},{2,6},{6,10},{10,14},{3,7},{... | collective-permute-start | bytes 780296 | tf_op jit(solution)/shard_map/ppermute | solution.py:12
  398.7 1.8 copy-start.12
  415.7 1.0 copy-start.6
  415.7 1.2 copy-start.8
  497.4 9.8 %copy-start.1 = (bf16[512,1024]{1,0:T(8,128)(2,1)S(1)}, bf16[512,1024]{1,0:T(8,128)(2,1)}, u32[]{:S(2)}) copy-start(bf16[512,1024]{1,0:T(8,128)(2,1)} %param.7) | copy-start | bytes 3145732
Sparse Core Ops, SparseCore 0:
  56.8 79.4 all-gather.9
  138.1 85.6 all-gather.7
  281.0 80.5 all-gather.11
  415.8 81.5 all-gather.13
where the time goes:
time: 521 us; the launch traced here: 514 us
  waiting for transfers between devices  335 us (64%)
  matrix products  78.3 us (15%)
  blocking collectives  34.5 us (7%)
  starting transfers between devices  27.9 us (5%)
  local copies, waits for them, and re-layouts  18 us (3%)
  between operations  13.9 us (3%)
  other arithmetic  6.4 us (1%)
    all_gather x3, waiting for transfers between devices, mixer_layer(): lax.all_gather(a, 'mp', axis=1, tiled=True)  239 us
    all_gather x1, waiting for transfers between devices, local(): weight_cols = lax.all_gather(out_weight, 'seq', axis=1, tiled=True)[0]  87.5 us
    conv_general_dilated x12, matrix products, depthwise(): lax.conv_general_dilated(extended[None], kernel, (1,), 'VALID', dimension...  51.1 us
    psum x3, blocking collectives, mixer_layer(): all_squares = lax.psum(own_squares, 'mp')  34.5 us
    ppermute x8, starting transfers between devices, passed_along(): return lax.ppermute(value, axis, pairs)  27.2 us
    dot_general x3, matrix products, mixer_layer(): jnp.dot(piece, block_rows, preferred_element_type=jnp.float32)  26 us
  transfers between devices with their start and end apart: 12, of which 10 were waited for; matrix products, arithmetic and copies ran while one was open for 2% of the time, Pallas kernels for 0%

commit v1 on v0

--- a/solution.py
+++ b/solution.py
@@ -27,10 +27,21 @@
 
 
 def mixer_layer(stream_in, gain, shorts, medium, weight_cols):
+
+    def load_tracks(vec):
+        workers = lax.axis_size("mp")
+        f_next = vec
+        for ix in [
+            [(idx, idx ^ at) for idx in range(workers)] for at in (1, 2, 4, 8, 16) if at < workers
+        ]:
+            part_now = lax.ppermute(f_next, axis_name="mp", perm=ix)
+            f_next = f_next + part_now
+        return f_next
+
     rows = stream_in.shape[0]
     stream = stream_in.astype(jnp.float32)
     own_squares = jnp.sum(stream * stream, axis=1, keepdims=True)
-    all_squares = lax.psum(own_squares, "mp")
+    all_squares = load_tracks(own_squares)
     normed = (
         stream * lax.rsqrt(all_squares / D + 1e-06) * gain.astype(jnp.float32)[None, :]
     ).astype(jnp.bfloat16)

time: 521 us -> 517 us (level)
  blocking collectives: 34.5 us -> 0 us
  waiting for transfers between devices: 335 us -> 353 us
  starting transfers between devices: 27.9 us -> 41.1 us
    psum x3 -> x0, blocking collectives: 34.5 us -> none  [mixer_layer(): all_squares = lax.psum(own_squares, 'mp')]
    ppermute x0 -> x6, waiting for transfers between devices: none -> 13.1 us  [load_tracks(): part_now = lax.ppermute(f_next, axis_name='mp', perm=ix)]
    ppermute x0 -> x6, starting transfers between devices: none -> 12.3 us  [load_tracks(): part_now = lax.ppermute(f_next, axis_name='mp', perm=ix)]
  transfers between devices with their start and end apart: 12 -> 18, of which waited for: 10 -> 16; matrix products, arithmetic and copies ran while one was open for 2% -> 2% of each run, Pallas kernels for 0% -> 0%
where the time goes in v1:
time: 517 us; the launch traced here: 510 us
  waiting for transfers between devices  353 us (68%)
  matrix products  78.3 us (15%)
  starting transfers between devices  41.1 us (8%)
  local copies, waits for them, and re-layouts  18.4 us (4%)
  between operations  13.9 us (3%)
  other arithmetic  5.71 us (1%)
    all_gather x3, waiting for transfers between devices, mixer_layer(): lax.all_gather(a, 'mp', axis=1, tiled=True)  244 us
    all_gather x1, waiting for transfers between devices, local(): weight_cols = lax.all_gather(out_weight, 'seq', axis=1, tiled=True)[0]  87.5 us
    conv_general_dilated x12, matrix products, depthwise(): lax.conv_general_dilated(extended[None], kernel, (1,), 'VALID', dimension...  51.1 us
    ppermute x8, starting transfers between devices, passed_along(): return lax.ppermute(value, axis, pairs)  28 us
    dot_general x3, matrix products, mixer_layer(): jnp.dot(piece, block_rows, preferred_element_type=jnp.float32)  26 us
    ppermute x6, waiting for transfers between devices, load_tracks(): part_now = lax.ppermute(f_next, axis_name='mp', perm=ix)  13.1 us
    ppermute x6, starting transfers between devices, load_tracks(): part_now = lax.ppermute(f_next, axis_name='mp', perm=ix)  12.3 us
  transfers between devices with their start and end apart: 18, of which 16 were waited for; matrix products, arithmetic and copies ran while one was open for 2% of the time, Pallas kernels for 0%

profile of v1, /device:TPU:0, one launch (start us, length us, event | category | flops | bytes accessed | tf_op | source)
XLA Modules:
  0.0 510.4 jit_solution(7344661634316912493)
XLA Ops:
  6.5 0.8 fusion.139
  7.8 0.6 fusion.101
  8.4 3.1 collective-permute-start
  11.5 1.6 collective-permute-done
  13.0 3.0 collective-permute-start.1
  16.1 1.5 collective-permute-done.1
  17.8 3.7 collective-permute-start.2
  22.4 2.6 rev.25
  25.9 0.6 fusion.25
  26.5 0.7 fusion.23
  27.6 0.8 slice_bitcast_fusion.5
  28.4 4.1 collective-permute-start.3
  32.5 0.6 fusion.19
  33.1 0.6 copy.28
  33.7 2.3 reshape.126
  36.1 1.2 maximum_bitcast_fusion.1
  37.4 15.2 %fusion.86 = bf16[1,256,1024]{2,0,1:T(2,128)(2,1)} fusion(bf16[1,383,1024]{2,1,0:T(8,128)(2,1)S(1)} %maximum_bitcast_fusion.1, f32[1,264,1024]{2,0,1:T(1,128)S(1)} %copy-done.2, bf16[128,1,1024]{2,0,1:T(8,128)(2,1)S(1)} %bitcast.116), kind=kOutput, calls=%fused_computation.73 | convolution fusion | flops 67633152 | bytes 2619392 | tf_op jit(solution)/shard_map/conv_general_dilated | solution.py:17
  52.6 0.7 all-gather.8.cloned.1.call-update
  53.3 0.5 all-gather.12.cloned.1.call-start
  53.8 81.4 %all-gather.10.cloned.1.call-done = bf16[1,256,4096]{2,0,1:T(2,128)(2,1)} async-done(((bf16[1,256,1024]{2,0,1:T(2,128)(2,1)}), bf16[1,256,4096]{2,0,1:T(2,128)(2,1)}) %all-gather.10.cloned.1.call-update) | async-done | bytes 2097168 | tf_op jit(solution)/shard_map/all_gather | solution.py:61
  135.2 87.5 %all-gather.8.cloned.1.call-done = bf16[1,4096,1024]{2,1,0:T(8,128)(2,1)} async-done(((bf16[1,1024,1024]{2,1,0:T(8,128)(2,1)}), bf16[1,4096,1024]{2,1,0:T(8,128)(2,1)}) %all-gather.8.cloned.1.call-update) | async-done | bytes 8388624 | tf_op jit(solution)/shard_map/all_gather | solution.py:69
  222.8 8.6 %fusion.54 = bf16[256,1024]{1,0:T(8,128)(2,1)S(1)} fusion(bf16[1,4096,1024]{2,1,0:T(8,128)(2,1)} %all-gather.8.cloned.1.call-done, bf16[1,256,4096]{2,0,1:T(2,128)(2,1)} %all-gather.10.cloned.1.call-done, bf16[256,1024]{1,0:T(8,128)(2,1)S(1)} %get-tuple-element.15), kind=kOutput, calls=%fused_computation.62 | convolution fusion | flops 2148270080 | bytes 11534336 | tf_op jit(solution)/shard_map/dot_general | solution.py:63
  231.4 1.6 collective-permute-start.4
  233.0 1.5 collective-permute-done.4
  234.5 0.6 fusion.104
  235.1 1.6 collective-permute-start.5
  236.7 2.1 collective-permute-done.5
  238.7 2.4 collective-permute-start.6
  241.2 2.1 collective-permute-done.6
  243.4 3.4 collective-permute-start.7
  246.8 1.4 collective-permute-done.7
  249.0 0.6 fusion.33
  249.6 0.7 fusion.31
  250.7 0.8 slice_bitcast_fusion.4
  251.5 4.9 collective-permute-start.8
  256.4 0.6 fusion.27
  257.0 0.6 copy.38
  257.7 1.3 reshape.127
  259.0 0.9 collective-permute-done.8
  259.9 1.1 maximum_bitcast_fusion.2
  261.0 15.2 %fusion.92 = bf16[1,256,1024]{2,0,1:T(2,128)(2,1)} fusion(bf16[1,383,1024]{2,1,0:T(8,128)(2,1)S(1)} %maximum_bitcast_fusion.2, f32[1,264,1024]{2,0,1:T(1,128)S(1)} %reshape.127, bf16[128,1,1024]{2,0,1:T(8,128)(2,1)S(1)} %bitcast.117), kind=kOutput, calls=%fused_computation.75 | convolution fusion | flops 67633152 | bytes 2619392 | tf_op jit(solution)/shard_map/conv_general_dilated | solution.py:17
  276.4 83.3 %all-gather.12.cloned.1.call-done = bf16[1,256,4096]{2,0,1:T(2,128)(2,1)} async-done(((bf16[1,256,1024]{2,0,1:T(2,128)(2,1)}), bf16[1,256,4096]{2,0,1:T(2,128)(2,1)}) %all-gather.12.cloned.1.call-update) | async-done | bytes 2097168 | tf_op jit(solution)/shard_map/all_gather | solution.py:61
  359.7 8.6 %fusion.59 = bf16[256,1024]{1,0:T(8,128)(2,1)S(1)} fusion(bf16[1,4096,1024]{2,1,0:T(8,128)(2,1)} %all-gather.8.cloned.1.call-done, bf16[1,256,4096]{2,0,1:T(2,128)(2,1)} %all-gather.12.cloned.1.call-done, bf16[256,1024]{1,0:T(8,128)(2,1)S(1)} %copy-done.4), kind=kOutput, calls=%fused_computation.63 | convolution fusion | flops 2148270080 | bytes 11534336 | tf_op jit(solution)/shard_map/dot_general | solution.py:63
  368.4 1.3 collective-permute-start.9
  369.7 1.5 collective-permute-done.9
  371.5 3.6 collective-permute-done.10
  375.1 2.1 collective-permute-start.11
  377.2 2.3 collective-permute-done.11
  379.8 3.9 collective-permute-start.12
  383.7 1.4 collective-permute-done.12
  385.8 0.6 fusion.41
  386.4 0.7 fusion.39
  387.6 0.8 slice_bitcast_fusion.3
  388.4 5.1 %collective-permute-start.13 = (bf16[127,1024]{1,0:T(8,128)(2,1)}, bf16[127,1024]{1,0:T(8,128)(2,1)}, u32[]{:S(2)}, u32[]{:S(2)}) collective-permute-start(bf16[127,1024]{1,0:T(8,128)(2,1)} %slice_bitcast_fusion.3), channel_id=1, source_target_pairs={{0,4},{4,8},{8,12},{1,5},{5,9},{9,13},{2,6},{6,10},{10,14},{3,7},{... | collective-permute-start | bytes 780296 | tf_op jit(solution)/shard_map/ppermute | solution.py:12
  393.5 0.6 fusion.35
  394.1 0.6 copy.48
  394.7 1.3 reshape.128
  396.1 0.7 collective-permute-done.13
  396.8 1.1 maximum_bitcast_fusion.3
  397.9 15.2 %fusion.98 = bf16[1,256,1024]{2,0,1:T(2,128)(2,1)} fusion(bf16[1,383,1024]{2,1,0:T(8,128)(2,1)S(1)} %maximum_bitcast_fusion.3, f32[1,264,1024]{2,0,1:T(1,128)S(1)} %reshape.128, bf16[128,1,1024]{2,0,1:T(8,128)(2,1)S(1)} %bitcast.118), kind=kOutput, calls=%fused_computation.77 | convolution fusion | flops 67633152 | bytes 2619392 | tf_op jit(solution)/shard_map/conv_general_dilated | solution.py:17
  413.1 1.0 copy-done.6
  414.3 79.5 %all-gather.14.cloned.1.call-done = bf16[1,256,4096]{2,0,1:T(2,128)(2,1)} async-done(((bf16[1,256,1024]{2,0,1:T(2,128)(2,1)}), bf16[1,256,4096]{2,0,1:T(2,128)(2,1)}) %all-gather.14.cloned.1.call-update) | async-done | bytes 2097168 | tf_op jit(solution)/shard_map/all_gather | solution.py:61
  493.8 8.7 %fusion.78 = bf16[1,256,1024]{2,1,0:T(8,128)(2,1)S(1)} fusion(bf16[256,1024]{1,0:T(8,128)(2,1)S(1)} %copy-done.8, bf16[1,4096,1024]{2,1,0:T(8,128)(2,1)} %all-gather.8.cloned.1.call-done, bf16[1,256,4096]{2,0,1:T(2,128)(2,1)} %all-gather.14.cloned.1.call-done, bf16[256,1024]{1,0:T(8,128)(2,1)S(1)} %get-tuple-element.6, pred[]{:T(512)S(6)} %eq.14), kind=kOutput, calls=%fused_computation.71 | convolution fusion | flops 2148532224 | bytes 12058625 | tf_op jit(solution)/shard_map/dot_general | solution.py:63
  502.5 1.1 maximum_bitcast_fusion
  (83 shorter events, 6.6 us)
Async XLA Ops:
  6.5 1.3 copy-start
  6.5 9.5 %copy-start.14 = (bf16[1,1024]{1,0:T(2,128)(2,1)S(1)}, bf16[1,1024]{1,0:T(2,128)(2,1)}, u32[]{:S(2)}) copy-start(bf16[1,1024]{1,0:T(2,128)(2,1)} %param.8) | copy-start | bytes 6148
  6.5 128.7 %all-gather.10.cloned.1.call-start = ((), (), s32[]{:S(2)}) async-start(), calls=%async_computation.1 | async-start | bytes 5242880 | tf_op jit(solution)/shard_map/all_gather | solution.py:61
  7.8 13.8 %copy-start.13 = (bf16[1,3,7,1024]{3,2,1,0:T(8,128)(2,1)S(1)}, bf16[1,3,7,1024]{3,2,1,0:T(8,128)(2,1)}, u32[]{:S(2)}) copy-start(bf16[1,3,7,1024]{3,2,1,0:T(8,128)(2,1)} %param.9) | copy-start | bytes 129028
  8.4 14.0 %copy-start.9 = (bf16[1,128,1024]{2,1,0:T(8,128)(2,1)S(1)}, bf16[1,128,1024]{2,1,0:T(8,128)(2,1)}, u32[]{:S(2)}) copy-start(bf16[1,128,1024]{2,1,0:T(8,128)(2,1)} %param.10) | copy-start | bytes 786436
  8.4 4.7 collective-permute-start
  13.0 4.6 collective-permute-start.1
  17.8 7.1 %collective-permute-start.2 = (bf16[6,1024]{1,0:T(8,128)(2,1)S(1)}, bf16[6,1024]{1,0:T(8,128)(2,1)S(1)}, u32[]{:S(2)}, u32[]{:S(2)}) collective-permute-start(bf16[6,1024]{1,0:T(8,128)(2,1)S(1)} %slice.84), channel_id=1, source_target_pairs={{0,4},{4,8},{8,12},{1,5},{5,9},{9,13},{2,6},{6,10},{10,14},{3,7},{... | collective-permute-start | bytes 36872 | tf_op jit(solution)/shard_map/ppermute | solution.py:12
  25.2 0.7 copy-start.15
  28.4 7.7 %collective-permute-start.3 = (bf16[127,1024]{1,0:T(8,128)(2,1)}, bf16[127,1024]{1,0:T(8,128)(2,1)}, u32[]{:S(2)}, u32[]{:S(2)}) collective-permute-start(bf16[127,1024]{1,0:T(8,128)(2,1)} %slice_bitcast_fusion.5), channel_id=1, source_target_pairs={{0,4},{4,8},{8,12},{1,5},{5,9},{9,13},{2,6},{6,10},{10,14},{3,7},{... | collective-permute-start | bytes 780296 | tf_op jit(solution)/shard_map/ppermute | solution.py:12
  36.0 1.3 copy-start.2
  36.0 1.4 copy-start.10
  52.6 170.2 %all-gather.8.cloned.1.call-start = ((), (), s32[]{:S(2)}) async-start(), calls=%async_computation | async-start | bytes 10485760 | tf_op jit(solution)/shard_map/all_gather | solution.py:69
  53.3 306.4 %all-gather.12.cloned.1.call-start = ((), (), s32[]{:S(2)}) async-start(), calls=%async_computation.2 | async-start | bytes 5242880 | tf_op jit(solution)/shard_map/all_gather | solution.py:61
  231.4 3.1 copy-start.5
  231.4 3.1 collective-permute-start.4
  235.1 13.1 %copy-start.3 = (bf16[256,1024]{1,0:T(8,128)(2,1)}, bf16[256,1024]{1,0:T(8,128)(2,1)S(1)}, u32[]{:S(2)}) copy-start(bf16[256,1024]{1,0:T(8,128)(2,1)S(1)} %get-tuple-element.8) | copy-start | bytes 1572868
  235.1 3.6 collective-permute-start.5
  238.7 4.5 collective-permute-start.6
  243.4 4.8 collective-permute-start.7
  251.5 8.4 %collective-permute-start.8 = (bf16[127,1024]{1,0:T(8,128)(2,1)}, bf16[127,1024]{1,0:T(8,128)(2,1)}, u32[]{:S(2)}, u32[]{:S(2)}) collective-permute-start(bf16[127,1024]{1,0:T(8,128)(2,1)} %slice_bitcast_fusion.4), channel_id=1, source_target_pairs={{0,4},{4,8},{8,12},{1,5},{5,9},{9,13},{2,6},{6,10},{10,14},{3,7},{... | collective-permute-start | bytes 780296 | tf_op jit(solution)/shard_map/ppermute | solution.py:12
  259.0 2.0 copy-start.11
  261.0 98.7 %copy-start.4 = (bf16[256,1024]{1,0:T(8,128)(2,1)S(1)}, bf16[256,1024]{1,0:T(8,128)(2,1)}, u32[]{:S(2)}) copy-start(bf16[256,1024]{1,0:T(8,128)(2,1)} %copy-done.3) | copy-start | bytes 1572868
  276.2 217.6 %all-gather.14.cloned.1.call-start = ((), (), s32[]{:S(2)}) async-start(), calls=%async_computation.3 | async-start | bytes 5242880 | tf_op jit(solution)/shard_map/all_gather | solution.py:61
  368.3 11.4 %copy-start.7 = (bf16[256,1024]{1,0:T(8,128)(2,1)}, bf16[256,1024]{1,0:T(8,128)(2,1)S(1)}, u32[]{:S(2)}) copy-start(bf16[256,1024]{1,0:T(8,128)(2,1)S(1)} %fusion.59) | copy-start | bytes 1572868
  368.4 2.8 collective-permute-start.9
  371.4 3.6 collective-permute-start.10
  375.1 4.5 collective-permute-start.11
  379.8 5.3 %collective-permute-start.12 = (bf16[6,1024]{1,0:T(8,128)(2,1)S(1)}, bf16[6,1024]{1,0:T(8,128)(2,1)S(1)}, u32[]{:S(2)}, u32[]{:S(2)}) collective-permute-start(bf16[6,1024]{1,0:T(8,128)(2,1)S(1)} %slice.94), channel_id=1, source_target_pairs={{0,4},{4,8},{8,12},{1,5},{5,9},{9,13},{2,6},{6,10},{10,14},{3,7},{... | collective-permute-start | bytes 36872 | tf_op jit(solution)/shard_map/ppermute | solution.py:12
  388.4 8.4 %collective-permute-start.13 = (bf16[127,1024]{1,0:T(8,128)(2,1)}, bf16[127,1024]{1,0:T(8,128)(2,1)}, u32[]{:S(2)}, u32[]{:S(2)}) collective-permute-start(bf16[127,1024]{1,0:T(8,128)(2,1)} %slice_bitcast_fusion.3), channel_id=1, source_target_pairs={{0,4},{4,8},{8,12},{1,5},{5,9},{9,13},{2,6},{6,10},{10,14},{3,7},{... | collective-permute-start | bytes 780296 | tf_op jit(solution)/shard_map/ppermute | solution.py:12
  396.0 1.8 copy-start.12
  413.0 1.0 copy-start.6
  413.0 1.2 copy-start.8
  493.8 9.8 %copy-start.1 = (bf16[512,1024]{1,0:T(8,128)(2,1)S(1)}, bf16[512,1024]{1,0:T(8,128)(2,1)}, u32[]{:S(2)}) copy-start(bf16[512,1024]{1,0:T(8,128)(2,1)} %param.7) | copy-start | bytes 3145732
Sparse Core Ops, SparseCore 0:
  52.7 82.4 all-gather.9
  137.0 85.6 all-gather.7
  276.3 83.3 all-gather.11
  413.2 80.5 all-gather.13
